TPU v7x, 32 devices: a whole 2x2x4 slice. The times are simulated.
32 devices in a mesh: gx: 4 (over y, x), gy: 8 (over z, core).
Axes of the slice: x: 2, y: 2, z: 4, core: 2. Of those that a mesh axis runs over, the one named last changes fastest.
Arguments:
- u_wind: float32 [64, 64, 1024], P(None, 'gx', 'gy'), may hold values from -6 to 6
- v_wind: float32 [64, 64, 1024], P(None, 'gx', 'gy'), may hold values from -6 to 6
- w_wind: float32 [64, 64, 1024], P(None, 'gx', 'gy'), may hold values from -4 to 4
- pressure: float32 [64, 64, 1024], P(None, 'gx', 'gy'), may hold values from -6 to 6
- terrain_level: int32 [64, 1024], P('gx', 'gy'), may hold values from 0 to 8
- zone_width: int32 [4], replicated, may hold values from 5 to 16
- stiffness: float32 [64], replicated, may hold values from 0.25 to 2
- inflow_profile: float32 [2, 64], replicated, may hold values from -5 to 5
Outputs:
- u_final: float32 [64, 64, 1024], P(None, 'gx', 'gy')
- v_final: float32 [64, 64, 1024], P(None, 'gx', 'gy')
- w_final: float32 [64, 64, 1024], P(None, 'gx', 'gy')
- p_final: float32 [64, 64, 1024], P(None, 'gx', 'gy')
Inputs may be any that keep to these rules, and one draw needn't show every extreme that they name: `zone_width`: zone widths in columns.
All inputs are finite; a program needn't handle non-finite values.
Results may differ from a plain program's by a relative error of at most 0.0001.
Values sent between devices are 32-bit elements; how exact they have to be, the bound alone decides.
A program may use at most 128 MiB of HBM per device.

v0:
```python
import functools

import jax
import jax.numpy as jnp
from jax import lax
from jax.experimental import pallas as pl
from jax.experimental.pallas import tpu as pltpu
from jax.sharding import PartitionSpec as P

SUB = 6
ADV = 0.3
HC = 0.4
ZC = 1.0
RELAX = 0.5
EXT = 32
LO = 8
DRY = 1 << 20
WEST, EAST, SOUTH, NORTH = 0, 1, 2, 3
CHUNK = 4


def stencil(c, m3, m2, m1, f0, e1, e2):
    centered = 37.0 * (f0 + m1) - 8.0 * (e1 + m2) + (e2 + m3)
    upwind = 10.0 * (f0 - m1) - 5.0 * (e1 - m2) + (e2 - m3)
    return c * centered - jnp.abs(c) * upwind


def kernel(
    nz,
    bx,
    cnt,
    u_in,
    v_in,
    w_in,
    p_in,
    terr,
    zone,
    g,
    prof,
    u_out,
    v_out,
    w_out,
    p_out,
    u_ext,
    v_ext,
    w_ext,
    p_ext,
    tend,
    q_buf,
    d_buf,
    w_buf,
    cc,
    li,
    wi,
    xs,
    xr,
    ys,
    yr,
    g_lo,
    g_hi,
    trx,
    tr_y,
    terr_ext,
    ps_x,
    pr_x,
    ps_y,
    pr_y,
    us_x,
    ur_x,
    vs_y,
    vr_y,
    ub_x,
    wet_x,
    uh_x,
    ini_s,
    ini_r,
    ter_s,
    ter_r,
    uv_s,
    uv_r,
    stp_s,
    stp_r,
):
    by = 128
    gx = lax.axis_index("gx")
    gy = lax.axis_index("gy")
    nx_dev, ny_dev = cnt
    has = (gx > 0, gx < nx_dev - 1, gy > 0, gy < ny_dev - 1)
    peer = ({"gx": gx - 1}, {"gx": gx + 1}, {"gy": gy - 1}, {"gy": gy + 1})
    opp = (EAST, WEST, NORTH, SOUTH)
    exts = (u_ext, v_ext, w_ext, p_ext)
    ins = (u_in, v_in, w_in, p_in)

    barrier = pltpu.get_barrier_semaphore()
    for d in range(4):

        @pl.when(has[d])
        def _(d=d):
            pl.semaphore_signal(
                barrier, inc=1, device_id=peer[d], device_id_type=pl.DeviceIdType.MESH
            )

    def rcopy(d, src, dst, ss, rs):
        return pltpu.make_async_remote_copy(
            src_ref=src,
            dst_ref=dst,
            send_sem=ss,
            recv_sem=rs,
            device_id=peer[d],
            device_id_type=pl.DeviceIdType.MESH,
        )

    def start(d, *args):
        @pl.when(has[d])
        def _():
            rcopy(d, *args).start()

    def wait_send(d, *args):
        @pl.when(has[d])
        def _():
            rcopy(d, *args).wait_send()

    def wait_recv(d, *args):
        @pl.when(has[opp[d]])
        def _():
            rcopy(d, *args).wait_recv()

    def ini(d, f):
        if d < 2:
            return xs.at[d, f], xr.at[d, f], ini_s.at[d, f], ini_r.at[d, f]
        return ys.at[d - 2, f], yr.at[d - 2, f], ini_s.at[d, f], ini_r.at[d, f]

    def ter(d):
        if d == WEST:
            return terr.at[pl.ds(0, 8)], trx, ter_s.at[0], ter_r.at[0]
        return terr, tr_y, ter_s.at[1], ter_r.at[1]

    def uv(d):
        if d == WEST:
            return us_x, ur_x, uv_s.at[0], uv_r.at[0]
        return vs_y, vr_y, uv_s.at[1], uv_r.at[1]

    def stp(d, s):
        if d < 2:
            return ps_x.at[d, s], pr_x.at[d, s], stp_s.at[d, s], stp_r.at[d, s]
        return ps_y.at[s], pr_y.at[d - 2, s], stp_s.at[d, s], stp_r.at[d, s]

    rows = lax.broadcasted_iota(jnp.int32, (bx, by), 0)
    lane = lax.broadcasted_iota(jnp.int32, (bx, by), 1)

    def slab(k):
        return pl.ds(pl.multiple_of(k * bx, bx), bx)

    def ext_at(k, off, n):
        return pl.ds(k * EXT + off, n)

    def own(k):
        return pl.ds(pl.multiple_of(k * EXT + LO, 8), bx)

    def edge(ref, off):
        return [ref[pl.ds(k * EXT + off, 8, stride=EXT), :] for k in range(0, nz, 8)]

    for d in range(4):

        @pl.when(jnp.logical_not(has[opp[d]]))
        def _(d=d):
            if d < 2:
                xr[d] = jnp.zeros(xr.shape[1:], jnp.float32)
                pr_x[d] = jnp.zeros(pr_x.shape[1:], jnp.float32)
            else:
                yr[d - 2] = jnp.zeros(yr.shape[1:], jnp.float32)
                pr_y[d - 2] = jnp.zeros(pr_y.shape[1:], jnp.float32)
            if d == WEST:
                trx[...] = jnp.full(trx.shape, DRY, jnp.int32)
                ur_x[...] = jnp.zeros(ur_x.shape, jnp.float32)
            if d == SOUTH:
                tr_y[...] = jnp.full(tr_y.shape, DRY, jnp.int32)
                vr_y[...] = jnp.zeros(vr_y.shape, jnp.float32)

    neighbours = sum(h.astype(jnp.int32) for h in has)
    pl.semaphore_wait(barrier, neighbours)
    start(WEST, *ter(WEST))
    start(SOUTH, *ter(SOUTH))

    for f in range(4):
        for r in range(3):
            for k in range(0, nz, 8):
                xs[WEST, f, pl.ds(r * nz + k, 8), :] = ins[f][pl.ds(k * bx + r, 8, stride=bx), :]
                xs[EAST, f, pl.ds(r * nz + k, 8), :] = ins[f][
                    pl.ds(k * bx + bx - 3 + r, 8, stride=bx), :
                ]
        start(WEST, *ini(WEST, f))
        start(EAST, *ini(EAST, f))

    group = by // 8
    for f in range(4):

        def pack(kg, carry, f=f):
            lo = hi = jnp.zeros((bx, by), jnp.float32)
            for kk in range(group):
                k = kg * group + kk
                x = ins[f][slab(k), :]
                exts[f][own(k), :] = x
                pick = (lane >> 3) == kk
                lo = jnp.where(pick, pltpu.roll(x, 8 * kk + 3, 1), lo)
                hi = jnp.where(pick, pltpu.roll(x, 8 * kk + 5, 1), hi)
            ys[SOUTH - 2, f, slab(kg), :] = lo
            ys[NORTH - 2, f, slab(kg), :] = hi
            return carry

        lax.fori_loop(0, nz // group, pack, 0)
        start(SOUTH, *ini(SOUTH, f))
        start(NORTH, *ini(NORTH, f))

    def relax_of(ci, rj):
        best = None
        for n, dist in enumerate(
            (
                ci,
                (nx_dev * bx - 1.0) - ci,
                rj,
                (ny_dev * by - 1.0) - rj,
            )
        ):
            width = jnp.full(ci.shape, zone[n], jnp.int32).astype(jnp.float32)
            ramp = jnp.maximum(width - dist, 0.0) / width
            best = ramp if best is None else jnp.maximum(best, ramp)
        return RELAX * best

    start_x = gx * bx
    start_y = gy * by
    ci = (rows + start_x).astype(jnp.float32)
    rj = (lane + start_y).astype(jnp.float32)
    relax = relax_of(ci, rj)
    keep = 1.0 - relax
    relax_hx = relax_of(
        (jnp.zeros((8, by), jnp.int32) + (start_x + bx)).astype(jnp.float32), rj[:8]
    )
    relax_hy = relax_of(ci, (jnp.zeros((bx, by), jnp.int32) + (start_y + by)).astype(jnp.float32))

    zero = jnp.zeros((bx, by), jnp.float32)
    for ref in (cc, li, wi, d_buf, w_buf):
        ref[pl.ds(0, bx), :] = zero
    t0 = terr[...]

    def coeff(k, carry):
        c_prev, vrow = carry
        above = jnp.minimum(k + 1, nz - 1)
        wet = jnp.where(t0 <= k, 1.0, 0.0)
        wet_b = jnp.where(jnp.logical_and(t0 <= k - 1, rows + k > rows), 1.0, 0.0)
        wet_a = jnp.where(jnp.logical_and(t0 <= k + 1, rows + (k + 1) < rows + nz), 1.0, 0.0)
        gk = (ZC * ZC) * g[k] * wet
        ga = (ZC * ZC) * g[above] * wet_a
        low = -gk * wet_b
        up = -ga * wet
        inv = 1.0 / (1.0 + wet * (ga + gk) - low * c_prev)
        c_new = up * inv
        cc[slab(k + 1), :] = c_new
        li[slab(k + 1), :] = low * inv
        wi[slab(k + 1), :] = wet * inv
        ub_x[pl.ds(k, 1), :] = jnp.full((1, by), prof[0, k], jnp.float32)
        vrow = jnp.where((lane >> 1) == k, prof[1, k], vrow)
        return c_new, vrow

    _, vb_y = lax.fori_loop(0, nz, coeff, (zero, zero))

    wait_recv(WEST, *ter(WEST))
    wait_recv(SOUTH, *ter(SOUTH))
    terr_ext[pl.ds(0, bx), :] = t0
    terr_ext[pl.ds(bx, 8), :] = trx[...]
    t1 = terr_ext[pl.ds(1, bx), :]
    t_east = jnp.broadcast_to(trx[0:1, :], (8, by))
    sub8 = lax.broadcasted_iota(jnp.int32, (8, by), 0)
    for k in range(0, nz, 8):
        wet_x[pl.ds(k, 8), :] = jnp.where(t_east <= sub8 + k, 1.0, 0.0)
    t_north = jnp.broadcast_to(tr_y[:, 0:1], (bx, by))
    wet_y = jnp.where(t_north <= (lane >> 1), 1.0, 0.0)

    scale = ADV / 60.0
    for f in range(4):
        wait_recv(SOUTH, *ini(SOUTH, f))
        wait_recv(NORTH, *ini(NORTH, f))

    def shifts(xw, xe):
        return (
            pltpu.roll(xw, 3, 1),
            pltpu.roll(xw, 2, 1),
            pltpu.roll(xw, 1, 1),
            xw,
            pltpu.roll(xe, by - 1, 1),
            pltpu.roll(xe, by - 2, 1),
        )

    def merge(kg, carry):
        at = slab(kg)

        def low(f):
            return jnp.where(
                (lane & 7) < 3,
                pltpu.roll(yr[NORTH - 2, f, at, :], by - 2, 1),
                ys[SOUTH - 2, f, at, :],
            )

        def high(f):
            return jnp.where(
                (lane & 7) < 5, ys[NORTH - 2, f, at, :], pltpu.roll(yr[SOUTH - 2, f, at, :], 2, 1)
            )

        c_lo = low(1) * scale
        c_hi = high(1) * scale
        for f in range(4):
            x = low(f)
            g_lo[f, at, :] = stencil(c_lo, *shifts(x, x))
            x = high(f)
            g_hi[f, at, :] = stencil(c_hi, *shifts(x, x))
        return carry

    lax.fori_loop(0, nz // group, merge, 0)

    def advect_y(k, carry):
        kg = k // group
        kk = k - kg * group
        c = v_ext[own(k), :] * scale
        for f in range(4):
            x = exts[f][own(k), :]
            lo = pltpu.roll(g_lo[f, slab(kg), :], by - 3 - 8 * kk, 1)
            hi = pltpu.roll(g_hi[f, slab(kg), :], by - 5 - 8 * kk, 1)
            flux = stencil(c, *shifts(x, x))
            flux = jnp.where(lane >= by - 2, hi, jnp.where(lane < 3, lo, flux))
            nxt = pltpu.roll(jnp.where(lane == 0, hi, flux), by - 1, 1)
            tend[f, slab(k), :] = x - (nxt - flux)
        return carry

    lax.fori_loop(0, nz, advect_y, 0, unroll=2)

    for f in range(4):
        wait_recv(WEST, *ini(WEST, f))
        wait_recv(EAST, *ini(EAST, f))
        for r in range(3):
            for k in range(0, nz, 8):
                exts[f][pl.ds(k * EXT + LO - 3 + r, 8, stride=EXT), :] = xr[
                    EAST, f, pl.ds(r * nz + k, 8), :
                ]
                exts[f][pl.ds(k * EXT + LO + bx + r, 8, stride=EXT), :] = xr[
                    WEST, f, pl.ds(r * nz + k, 8), :
                ]

    def advect_x(k, carry):
        acc_p, acc_v = carry
        n = bx + 8
        c = u_ext[ext_at(k, LO, n), :] * scale
        wet = t0 <= k
        res = []
        for f in range(4):
            sh = [exts[f][ext_at(k, LO + o, n), :] for o in (-3, -2, -1, 0, 1, 2)]
            flux = stencil(c, *sh)
            nxt = pltpu.roll(flux, n - 1, 0)[:bx]
            res.append(jnp.where(wet, tend[f, slab(k), :] - (nxt - flux[:bx]), 0.0))
        u_ext[own(k), :] = res[0]
        v_ext[own(k), :] = res[1]
        w_buf[slab(k + 1), :] = res[2]
        p_ext[own(k), :] = res[3]
        pick = (lane >> 1) == k
        acc_p = jnp.where(pick, pltpu.roll(res[3], 2 * k + 1, 1), acc_p)
        acc_v = jnp.where(pick, pltpu.roll(res[1], 2 * k + 1, 1), acc_v)
        return acc_p, acc_v

    acc_p, acc_v = lax.fori_loop(0, nz, advect_x, (zero, zero))

    def send_p(s, acc):
        for n, x in enumerate(edge(p_ext, LO)):
            ps_x[WEST, s, pl.ds(8 * n, 8), :] = x
        start(WEST, *stp(WEST, s))
        for n, x in enumerate(edge(p_ext, LO + bx - 1)):
            ps_x[EAST, s, pl.ds(8 * n, 8), :] = x
        start(EAST, *stp(EAST, s))
        ps_y[s] = acc
        start(SOUTH, *stp(SOUTH, s))
        start(NORTH, *stp(NORTH, s))

    vs_y[...] = acc_v
    start(SOUTH, *uv(SOUTH))
    for n, x in enumerate(edge(u_ext, LO)):
        us_x[pl.ds(8 * n, 8), :] = x
    start(WEST, *uv(WEST))
    send_p(0, acc_p)

    for f in range(4):
        for d in range(4):
            wait_send(d, *ini(d, f))
    for d in (WEST, SOUTH):
        wait_send(d, *ter(d))
        wait_send(d, *uv(d))
        wait_recv(d, *uv(d))
    uh_x[...] = ur_x[...]
    vh0 = pltpu.roll(vr_y[...], by - 1, 1)
    even = (lane & 1) == 0

    def substep(s, vh):
        for d in range(4):
            wait_recv(d, *stp(d, s))
        for k in range(0, nz, 8):
            at = pl.ds(k, 8)
            p_east = pr_x[WEST, s, at, :]
            p_ext[pl.ds(k * EXT + LO + bx, 8, stride=EXT), :] = p_east
            p_ext[pl.ds(k * EXT + LO - 1, 8, stride=EXT), :] = pr_x[EAST, s, at, :]
            uh = uh_x[at, :]
            u_ext[pl.ds(k * EXT + LO + bx, 8, stride=EXT), :] = uh
            wet = wet_x[at, :]
            un = wet * (uh - HC * (p_east - ps_x[EAST, s, at, :]))
            uh_x[at, :] = un - relax_hx * (un - wet * ub_x[at, :])
        vn_h = wet_y * (vh - HC * (pltpu.roll(pr_y[SOUTH - 2, s], by - 1, 1) - ps_y[s]))
        vh_next = vn_h - relax_hy * (vn_h - wet_y * vb_y)
        halo = jnp.where(even, vn_h, pltpu.roll(pr_y[NORTH - 2, s], 1, 1))

        def down(kc, carry):
            q_prev, d_prev = carry
            k0 = kc * CHUNK
            stores = []
            for i in range(CHUNK):
                k = k0 + i
                wet = t0 <= k
                p0 = p_ext[own(k), :]
                pm = p_ext[ext_at(k, LO - 1, bx), :]
                p1 = p_ext[ext_at(k, LO + 1, bx), :]
                un = jnp.where(wet, u_ext[own(k), :] - HC * (p0 - pm), 0.0)
                un1 = jnp.where(t1 <= k, u_ext[ext_at(k, LO + 1, bx), :] - HC * (p1 - p0), 0.0)
                hv = pltpu.roll(halo, by - 1 - 2 * k, 1)
                south = jnp.where(lane == 0, hv, pltpu.roll(p0, 1, 1))
                vn = jnp.where(wet, v_ext[own(k), :] - HC * (p0 - south), 0.0)
                vn1 = jnp.where(lane == by - 1, hv, pltpu.roll(vn, by - 1, 1))
                q = jnp.where(wet, p0 - (g[k] * HC) * ((un1 - un) + (vn1 - vn)), 0.0)
                d_new = (
                    wi[slab(k), :] * (w_buf[slab(k), :] - ZC * (q - q_prev)) - li[slab(k), :] * d_prev
                )
                u_rel = un - relax * (un - jnp.where(wet, prof[0, k], 0.0))
                v_rel = vn - relax * (vn - jnp.where(wet, prof[1, k], 0.0))
                stores.append((k, q, d_new, u_rel, v_rel))
                q_prev, d_prev = q, d_new
            for k, q, d_new, u_rel, v_rel in stores:
                q_buf[slab(k), :] = q
                d_buf[slab(k), :] = d_new
                u_ext[own(k), :] = u_rel
                v_ext[own(k), :] = v_rel
            return q_prev, d_prev

        q_last, d_last = lax.fori_loop(0, nz // CHUNK, down, (zero, zero))
        top = (
            wi[pl.ds(nz * bx, bx), :] * (w_buf[pl.ds(nz * bx, bx), :] + ZC * q_last)
            - li[pl.ds(nz * bx, bx), :] * d_last
        )

        def up(kc, carry):
            x, acc = carry
            k0 = nz - CHUNK - kc * CHUNK
            stores = []
            for i in range(CHUNK - 1, -1, -1):
                k = k0 + i
                below = d_buf[slab(k), :] - cc[slab(k), :] * x
                p = (q_buf[slab(k), :] - (g[k] * ZC) * (x - below)) * keep
                acc = jnp.where((lane >> 1) == k, pltpu.roll(p, (2 * k + 1), 1), acc)
                stores.append((k, p, x * keep))
                x = below
            for k, p, w in stores:
                p_ext[own(k), :] = p
                w_buf[slab(k + 1), :] = w
            return x, acc

        _, acc = lax.fori_loop(0, nz // CHUNK, up, (top, zero))

        for d in range(4):
            wait_send(d, *stp(d, s))

        @pl.when(s < SUB - 1)
        def _():
            send_p(s + 1, acc)

        return vh_next

    lax.fori_loop(0, SUB, substep, vh0)

    def finish(k, carry):
        u_out[slab(k), :] = u_ext[own(k), :]
        v_out[slab(k), :] = v_ext[own(k), :]
        w_out[slab(k), :] = w_buf[slab(k + 1), :]
        p_out[slab(k), :] = p_ext[own(k), :]
        return carry

    lax.fori_loop(0, nz, finish, 0, unroll=4)


def solution(mesh):
    cnt = (mesh.shape["gx"], mesh.shape["gy"])

    def on_device(u, v, w, p, terr, zone, g, prof):
        nz, bx, by = u.shape
        assert by == 128 and bx % 8 == 0 and 2 * nz == by
        flat = [a.reshape(nz * bx, by) for a in (u, v, w, p)]
        f32 = jnp.float32
        vm = pltpu.VMEM
        ext = vm((nz * EXT + 8, by), f32)
        lev = vm((nz * bx, by), f32)
        lev1 = vm(((nz + 1) * bx, by), f32)
        strip = nz * 8 * bx // by
        dma = pltpu.SemaphoreType.DMA
        scratch = [
            ext, ext, ext, ext,
            vm((4, nz * bx, by), f32),
            lev, lev1, lev1, lev1, lev1, lev1,
            vm((2, 4, 3 * nz, by), f32),
            vm((2, 4, 3 * nz, by), f32),
            vm((2, 4, strip, by), f32),
            vm((2, 4, strip, by), f32),
            vm((4, strip, by), f32),
            vm((4, strip, by), f32),
            vm((8, by), jnp.int32),
            vm((bx, by), jnp.int32),
            vm((bx + 8, by), jnp.int32),
            vm((2, SUB, nz, by), f32),
            vm((2, SUB, nz, by), f32),
            vm((SUB, bx, by), f32),
            vm((2, SUB, bx, by), f32),
            vm((nz, by), f32),
            vm((nz, by), f32),
            vm((bx, by), f32),
            vm((bx, by), f32),
            vm((nz, by), f32),
            vm((nz, by), f32),
            vm((nz, by), f32),
            dma((4, 4)), dma((4, 4)),
            dma((2,)), dma((2,)),
            dma((2,)), dma((2,)),
            dma((4, SUB)), dma((4, SUB)),
        ]
        vspec = pl.BlockSpec(memory_space=pltpu.VMEM)
        sspec = pl.BlockSpec(memory_space=pltpu.SMEM)
        outs = pl.pallas_call(
            functools.partial(kernel, nz, bx, cnt),
            out_shape=[jax.ShapeDtypeStruct((nz * bx, by), f32)] * 4,
            in_specs=[vspec] * 5 + [sspec] * 3,
            out_specs=[vspec] * 4,
            scratch_shapes=scratch,
            compiler_params=pltpu.CompilerParams(collective_id=0, has_side_effects=True),
        )(*flat, terr, zone, g, prof)
        return tuple(a.reshape(nz, bx, by) for a in outs)

    field = P(None, "gx", "gy")
    return jax.shard_map(
        on_device,
        mesh=mesh,
        in_specs=(field, field, field, field, P("gx", "gy"), P(), P(), P()),
        out_specs=(field,) * 4,
        check_vma=False,
    )
```

profile of v0, /device:TPU:0, one launch (start us, length us, event | category | flops | bytes accessed | tf_op | source)
XLA Modules:
  0.0 86.5 jit_solution(3123822162596738105)
XLA Ops:
  0.6 80.6 %shard_map.111 = (f32[1024,128]{1,0:T(8,128)}, f32[1024,128]{1,0:T(8,128)}, f32[1024,128]{1,0:T(8,128)}, f32[1024,128]{1,0:T(8,128)}) custom-call(f32[1024,128]{1,0:T(8,128)} %bitcast.8, f32[1024,128]{1,0:T(8,128)} %bitcast.9, f32[1024,128]{1,0:T(8,128)} %bitcast.10, f32[1024,128]{1,0:T(8,128)} %bitcast.11, s32[16,128]{1,0:T(8,128)} %terr.1, s32[4]{0:T(128)} %zone.1, ...), custom_call_target="tpu_custom_call" | custom-call | tf_op jit(solution)/shard_map/pallas_call | solution.py:537
  81.3 0.0 copy-start.2
  81.3 1.9 %copy.16 = f32[64,16,128]{2,1,0:T(8,128)} copy(f32[64,16,128]{2,1,0:T(8,128)} %bitcast.15) | data formatting | bytes 1048576
  83.2 0.0 copy-done.2
  83.2 0.0 copy-start.1
  83.2 0.8 copy.17
  84.0 0.4 copy-done.1
  84.4 0.0 copy-start
  84.4 0.8 copy.18
  85.2 0.4 copy-done
  85.7 0.8 copy.19
Async XLA Ops:
  81.3 1.9 %copy-start.2 = (f32[1024,128]{1,0:T(8,128)S(1)}, f32[1024,128]{1,0:T(8,128)}, u32[]{:S(2)}) copy-start(f32[1024,128]{1,0:T(8,128)} %get-tuple-element.9) | copy-start | bytes 1572868
  83.2 1.2 %copy-start.1 = (f32[1024,128]{1,0:T(8,128)S(1)}, f32[1024,128]{1,0:T(8,128)}, u32[]{:S(2)}) copy-start(f32[1024,128]{1,0:T(8,128)} %get-tuple-element.10) | copy-start | bytes 1572868
  84.4 1.2 %copy-start = (f32[1024,128]{1,0:T(8,128)S(1)}, f32[1024,128]{1,0:T(8,128)}, u32[]{:S(2)}) copy-start(f32[1024,128]{1,0:T(8,128)} %get-tuple-element.11) | copy-start | bytes 1572868
where the time goes:
time: 86.7 us; the launch traced here: 86.5 us
  Pallas kernels  80.6 us (93%)
  local copies, waits for them, and re-layouts  5.18 us (6%)
    pallas_call x1, Pallas kernels, on_device(): pl.pallas_call(functools.partial(kernel, nz, bx, cnt), out_shape=[jax.Sha...  80.6 us
    unnamed x10, local copies, waits for them, and re-layouts  5.18 us

commit v1 on v0

--- a/solution.py
+++ b/solution.py
@@ -16,7 +16,7 @@
 LO = 8
 DRY = 1 << 20
 WEST, EAST, SOUTH, NORTH = 0, 1, 2, 3
-CHUNK = 4
+CHUNK = 32
 
 
 def stencil(c, m3, m2, m1, f0, e1, e2):
@@ -365,7 +365,7 @@
         acc_v = jnp.where(pick, pltpu.roll(res[1], 2 * k + 1, 1), acc_v)
         return acc_p, acc_v
 
-    acc_p, acc_v = lax.fori_loop(0, nz, advect_x, (zero, zero))
+    acc_p, acc_v = lax.fori_loop(0, nz, advect_x, (zero, zero), unroll=4)
 
     def send_p(s, acc):
         for n, x in enumerate(edge(p_ext, LO)):

time: 86.7 us -> 66.9 us (0.77)
  Pallas kernels: 80.6 us -> 60.8 us
    pallas_call x1, Pallas kernels: 80.6 us -> 60.8 us  [on_device(): pl.pallas_call(functools.partial(kernel, nz, bx, cnt), out_shape=[jax.Sha...]
where the time goes in v1:
time: 66.9 us; the launch traced here: 66.6 us
  Pallas kernels  60.8 us (91%)
  local copies, waits for them, and re-layouts  5.18 us (8%)
    pallas_call x1, Pallas kernels, on_device(): pl.pallas_call(functools.partial(kernel, nz, bx, cnt), out_shape=[jax.Sha...  60.8 us
    unnamed x10, local copies, waits for them, and re-layouts  5.18 us

profile of v1, /device:TPU:0, one launch (start us, length us, event | category | flops | bytes accessed | tf_op | source)
XLA Modules:
  0.0 66.6 jit_solution(9408221332285360514)
XLA Ops:
  0.6 60.8 %shard_map.111 = (f32[1024,128]{1,0:T(8,128)}, f32[1024,128]{1,0:T(8,128)}, f32[1024,128]{1,0:T(8,128)}, f32[1024,128]{1,0:T(8,128)}) custom-call(f32[1024,128]{1,0:T(8,128)} %bitcast.8, f32[1024,128]{1,0:T(8,128)} %bitcast.9, f32[1024,128]{1,0:T(8,128)} %bitcast.10, f32[1024,128]{1,0:T(8,128)} %bitcast.11, s32[16,128]{1,0:T(8,128)} %terr.1, s32[4]{0:T(128)} %zone.1, ...), custom_call_target="tpu_custom_call" | custom-call | tf_op jit(solution)/shard_map/pallas_call | solution.py:537
  61.4 0.0 copy-start.2
  61.4 1.9 %copy.16 = f32[64,16,128]{2,1,0:T(8,128)} copy(f32[64,16,128]{2,1,0:T(8,128)} %bitcast.15) | data formatting | bytes 1048576
  63.3 0.0 copy-done.2
  63.4 0.0 copy-start.1
  63.4 0.8 %copy.17 = f32[64,16,128]{2,1,0:T(8,128)} copy(f32[64,16,128]{2,1,0:T(8,128)S(1)} %bitcast.14) | data formatting | bytes 1048576
  64.1 0.4 copy-done.1
  64.6 0.0 copy-start
  64.6 0.8 %copy.18 = f32[64,16,128]{2,1,0:T(8,128)} copy(f32[64,16,128]{2,1,0:T(8,128)S(1)} %bitcast.13) | data formatting | bytes 1048576
  65.4 0.4 copy-done
  65.8 0.8 %copy.19 = f32[64,16,128]{2,1,0:T(8,128)} copy(f32[64,16,128]{2,1,0:T(8,128)S(1)} %bitcast.12) | data formatting | bytes 1048576
Async XLA Ops:
  61.4 1.9 %copy-start.2 = (f32[1024,128]{1,0:T(8,128)S(1)}, f32[1024,128]{1,0:T(8,128)}, u32[]{:S(2)}) copy-start(f32[1024,128]{1,0:T(8,128)} %get-tuple-element.9) | copy-start | bytes 1572868
  63.4 1.2 %copy-start.1 = (f32[1024,128]{1,0:T(8,128)S(1)}, f32[1024,128]{1,0:T(8,128)}, u32[]{:S(2)}) copy-start(f32[1024,128]{1,0:T(8,128)} %get-tuple-element.10) | copy-start | bytes 1572868
  64.6 1.2 %copy-start = (f32[1024,128]{1,0:T(8,128)S(1)}, f32[1024,128]{1,0:T(8,128)}, u32[]{:S(2)}) copy-start(f32[1024,128]{1,0:T(8,128)} %get-tuple-element.11) | copy-start | bytes 1572868

commit v2 on v1

--- a/solution.py
+++ b/solution.py
@@ -140,10 +140,15 @@
             return us_x, ur_x, uv_s.at[0], uv_r.at[0]
         return vs_y, vr_y, uv_s.at[1], uv_r.at[1]
 
-    def stp(d, s):
+    def stp(d, s, h=0):
+        sems = stp_s.at[d, s, h], stp_r.at[d, s, h]
         if d < 2:
-            return ps_x.at[d, s], pr_x.at[d, s], stp_s.at[d, s], stp_r.at[d, s]
-        return ps_y.at[s], pr_y.at[d - 2, s], stp_s.at[d, s], stp_r.at[d, s]
+            part = pl.ds(h * CHUNK, CHUNK)
+            return ps_x.at[d, s, part], pr_x.at[d, s, part], *sems
+        return ps_y.at[s], pr_y.at[d - 2, s], *sems
+
+    def parts(d):
+        return range(nz // CHUNK if d < 2 else 1)
 
     rows = lax.broadcasted_iota(jnp.int32, (bx, by), 0)
     lane = lax.broadcasted_iota(jnp.int32, (bx, by), 1)
@@ -367,13 +372,13 @@
 
     acc_p, acc_v = lax.fori_loop(0, nz, advect_x, (zero, zero), unroll=4)
 
-    def send_p(s, acc):
-        for n, x in enumerate(edge(p_ext, LO)):
-            ps_x[WEST, s, pl.ds(8 * n, 8), :] = x
-        start(WEST, *stp(WEST, s))
-        for n, x in enumerate(edge(p_ext, LO + bx - 1)):
-            ps_x[EAST, s, pl.ds(8 * n, 8), :] = x
-        start(EAST, *stp(EAST, s))
+    def send_x(s, h):
+        for d, off in ((WEST, LO), (EAST, LO + bx - 1)):
+            for k in range(h * CHUNK, (h + 1) * CHUNK, 8):
+                ps_x[d, s, pl.ds(k, 8), :] = p_ext[pl.ds(k * EXT + off, 8, stride=EXT), :]
+            start(d, *stp(d, s, h))
+
+    def send_y(s, acc):
         ps_y[s] = acc
         start(SOUTH, *stp(SOUTH, s))
         start(NORTH, *stp(NORTH, s))
@@ -383,7 +388,9 @@
     for n, x in enumerate(edge(u_ext, LO)):
         us_x[pl.ds(8 * n, 8), :] = x
     start(WEST, *uv(WEST))
-    send_p(0, acc_p)
+    for h in range(nz // CHUNK):
+        send_x(0, h)
+    send_y(0, acc_p)
 
     for f in range(4):
         for d in range(4):
@@ -398,7 +405,8 @@
 
     def substep(s, vh):
         for d in range(4):
-            wait_recv(d, *stp(d, s))
+            for h in parts(d):
+                wait_recv(d, *stp(d, s, h))
         for k in range(0, nz, 8):
             at = pl.ds(k, 8)
             p_east = pr_x[WEST, s, at, :]
@@ -466,14 +474,23 @@
                 w_buf[slab(k + 1), :] = w
             return x, acc
 
-        _, acc = lax.fori_loop(0, nz // CHUNK, up, (top, zero))
+        carry = (top, zero)
+        for kc in range(nz // CHUNK):
+            carry = up(kc, carry)
+
+            @pl.when(s < SUB - 1)
+            def _(kc=kc):
+                send_x(s + 1, nz // CHUNK - 1 - kc)
+
+        acc = carry[1]
 
         for d in range(4):
-            wait_send(d, *stp(d, s))
+            for h in parts(d):
+                wait_send(d, *stp(d, s, h))
 
         @pl.when(s < SUB - 1)
         def _():
-            send_p(s + 1, acc)
+            send_y(s + 1, acc)
 
         return vh_next
 
@@ -530,7 +547,7 @@
             dma((4, 4)), dma((4, 4)),
             dma((2,)), dma((2,)),
             dma((2,)), dma((2,)),
-            dma((4, SUB)), dma((4, SUB)),
+            dma((4, SUB, nz // CHUNK)), dma((4, SUB, nz // CHUNK)),
         ]
         vspec = pl.BlockSpec(memory_space=pltpu.VMEM)
         sspec = pl.BlockSpec(memory_space=pltpu.SMEM)

time: 66.9 us -> 66.8 us (level)
  no operation moved by 1% of the time
where the time goes in v2:
time: 66.8 us; the launch traced here: 66.5 us
  Pallas kernels  60.6 us (91%)
  local copies, waits for them, and re-layouts  5.18 us (8%)
    pallas_call x1, Pallas kernels, on_device(): pl.pallas_call(functools.partial(kernel, nz, bx, cnt), out_shape=[jax.Sha...  60.6 us
    unnamed x10, local copies, waits for them, and re-layouts  5.18 us

profile of v2, /device:TPU:0, one launch (start us, length us, event | category | flops | bytes accessed | tf_op | source)
XLA Modules:
  0.0 66.5 jit_solution(16996666495094987116)
XLA Ops:
  0.6 60.6 %shard_map.111 = (f32[1024,128]{1,0:T(8,128)}, f32[1024,128]{1,0:T(8,128)}, f32[1024,128]{1,0:T(8,128)}, f32[1024,128]{1,0:T(8,128)}) custom-call(f32[1024,128]{1,0:T(8,128)} %bitcast.8, f32[1024,128]{1,0:T(8,128)} %bitcast.9, f32[1024,128]{1,0:T(8,128)} %bitcast.10, f32[1024,128]{1,0:T(8,128)} %bitcast.11, s32[16,128]{1,0:T(8,128)} %terr.1, s32[4]{0:T(128)} %zone.1, ...), custom_call_target="tpu_custom_call" | custom-call | tf_op jit(solution)/shard_map/pallas_call | solution.py:554
  61.3 0.0 copy-start.2
  61.3 1.9 %copy.16 = f32[64,16,128]{2,1,0:T(8,128)} copy(f32[64,16,128]{2,1,0:T(8,128)} %bitcast.15) | data formatting | bytes 1048576
  63.2 0.0 copy-done.2
  63.2 0.0 copy-start.1
  63.2 0.8 %copy.17 = f32[64,16,128]{2,1,0:T(8,128)} copy(f32[64,16,128]{2,1,0:T(8,128)S(1)} %bitcast.14) | data formatting | bytes 1048576
  64.0 0.4 copy-done.1
  64.5 0.0 copy-start
  64.5 0.8 %copy.18 = f32[64,16,128]{2,1,0:T(8,128)} copy(f32[64,16,128]{2,1,0:T(8,128)S(1)} %bitcast.13) | data formatting | bytes 1048576
  65.2 0.4 copy-done
  65.7 0.8 %copy.19 = f32[64,16,128]{2,1,0:T(8,128)} copy(f32[64,16,128]{2,1,0:T(8,128)S(1)} %bitcast.12) | data formatting | bytes 1048576
Async XLA Ops:
  61.3 1.9 %copy-start.2 = (f32[1024,128]{1,0:T(8,128)S(1)}, f32[1024,128]{1,0:T(8,128)}, u32[]{:S(2)}) copy-start(f32[1024,128]{1,0:T(8,128)} %get-tuple-element.9) | copy-start | bytes 1572868
  63.2 1.2 %copy-start.1 = (f32[1024,128]{1,0:T(8,128)S(1)}, f32[1024,128]{1,0:T(8,128)}, u32[]{:S(2)}) copy-start(f32[1024,128]{1,0:T(8,128)} %get-tuple-element.10) | copy-start | bytes 1572868
  64.5 1.2 %copy-start = (f32[1024,128]{1,0:T(8,128)S(1)}, f32[1024,128]{1,0:T(8,128)}, u32[]{:S(2)}) copy-start(f32[1024,128]{1,0:T(8,128)} %get-tuple-element.11) | copy-start | bytes 1572868
